TPU v7x, 32 devices: a whole 2x2x4 slice. The times are simulated.
32 devices in a mesh: pr: 8 (over y, x, core), pc: 4 (over z).
Axes of the slice: x: 2, y: 2, z: 4, core: 2. Of those that a mesh axis runs over, the one named last changes fastest.
Arguments:
- pair_array: bfloat16 [256, 256, 128], P('pr', 'pc'), may hold values from -6 to 6
- left_weight: bfloat16 [128, 128], replicated, may hold values from -0.5 to 0.5
- right_weight: bfloat16 [128, 128], replicated, may hold values from -0.5 to 0.5
- left_gate: bfloat16 [128, 128], replicated, may hold values from -0.5 to 0.5
- right_gate: bfloat16 [128, 128], replicated, may hold values from -0.5 to 0.5
- mid_gain: float32 [128], replicated, may hold values from 0.25 to 1.75
- out_weight: bfloat16 [128, 128], replicated, may hold values from -0.5 to 0.5
- out_gate: bfloat16 [128, 128], replicated, may hold values from -0.5 to 0.5
Outputs:
- pair_update: bfloat16 [256, 256, 128], P('pr', 'pc')
All inputs are finite; a program needn't handle non-finite values.
Results may differ from a plain program's by a relative error of at most 0.012.
Values may be sent and summed in bfloat16 or wider, within the bound.
A program may use at most 128 MiB of HBM per device.

v0:
```python
import jax
import jax.numpy as jnp
from jax import lax
from jax.sharding import PartitionSpec as P


def unit_channels(values, channel_gain):
    centred = values - jnp.mean(values, axis=-1, keepdims=True)
    return (
        centred
        * lax.rsqrt(jnp.mean(centred * centred, axis=-1, keepdims=True) + 1e-05)
        * channel_gain
    )


def make_factors(pair_in, left_weight, right_weight, left_gate, right_gate):
    left = jnp.einsum("ijc,cd->ijd", pair_in, left_weight, preferred_element_type=jnp.float32)
    left = left * jax.nn.sigmoid(
        jnp.einsum("ijc,cd->ijd", pair_in, left_gate, preferred_element_type=jnp.float32)
    )
    right = jnp.einsum("ijc,cd->ijd", pair_in, right_weight, preferred_element_type=jnp.float32)
    right = right * jax.nn.sigmoid(
        jnp.einsum("ijc,cd->ijd", pair_in, right_gate, preferred_element_type=jnp.float32)
    )
    return (pair_in, left.astype(jnp.bfloat16), right.astype(jnp.bfloat16))


def to_pair(mixed, ready, mid_gain, out_weight, out_gate):
    scaled = unit_channels(mixed.astype(jnp.float32), mid_gain).astype(jnp.bfloat16)
    scaled = lax.optimization_barrier(scaled)
    gate = jax.nn.sigmoid(
        jnp.einsum("ijc,cd->ijd", ready, out_gate, preferred_element_type=jnp.float32)
    )
    return (
        jnp.einsum("ijd,dc->ijc", scaled, out_weight, preferred_element_type=jnp.float32) * gate
    ).astype(jnp.bfloat16)


def on_device(
    pair_array, left_weight, right_weight, left_gate, right_gate, mid_gain, out_weight, out_gate
):
    ready, left, right = make_factors(pair_array, left_weight, right_weight, left_gate, right_gate)
    count = pair_array.shape[0] * lax.axis_size("pr")
    left_lines, right_lines = (
        lax.all_to_all(left, "pr", split_axis=2, concat_axis=0, tiled=True),
        lax.all_to_all(right, "pr", split_axis=2, concat_axis=0, tiled=True),
    )
    strip = jnp.einsum(
        "kid,kjd->ijd",
        lax.all_gather(left_lines, "pc", axis=1, tiled=True),
        right_lines,
        preferred_element_type=jnp.float32,
    )
    strip = (strip * count ** (-0.5)).astype(jnp.bfloat16)
    mixed = lax.all_to_all(strip, "pr", split_axis=0, concat_axis=2, tiled=True)
    return to_pair(mixed, ready, mid_gain, out_weight, out_gate)


def solution(mesh):
    return jax.shard_map(
        on_device,
        mesh=mesh,
        in_specs=(P("pr", "pc", None), P(), P(), P(), P(), P(), P(), P()),
        out_specs=P("pr", "pc", None),
        check_vma=False,
    )
```

profile of v0, /device:TPU:0, one launch (start us, length us, event | category | flops | bytes accessed | tf_op | source)
XLA Modules:
  0.0 104.0 jit_solution(1541400130074911763)
XLA Ops:
  6.5 0.0 copy-start
  6.5 0.0 all-gather.2.cloned.1.call-start
  6.5 1.0 copy-done
  7.6 1.0 fusion.24
  8.6 1.2 %fusion.14 = bf16[32,64,128]{2,1,0:T(8,128)(2,1)S(1)} fusion(f32[32,64,128]{2,1,0:T(8,128)S(1)} %fusion.24, bf16[32,64,128]{2,1,0:T(8,128)(2,1)S(1)} %copy-done, bf16[128,128]{1,0:T(8,128)(2,1)} %param.11), kind=kOutput, calls=%fused_computation.22 | convolution fusion | flops 68419584 | bytes 2129920 | tf_op jit(solution)/shard_map/ijc,cd->ijd/dot_general | solution.py:19
  9.8 1.6 %copy.25 = bf16[32,64,128]{1,0,2:T(8,128)(2,1)S(1)} copy(bf16[32,64,128]{2,1,0:T(8,128)(2,1)S(1)} %fusion.14) | data formatting | bytes 1048576 | tf_op jit(solution)/shard_map/convert_element_type | solution.py:25
  11.4 0.7 reshape.28
  12.2 14.7 %all_to_all.45 = bf16[8,2,16384]{2,1,0:T(2,128)(2,1)S(1)} all-to-all(bf16[8,2,16384]{2,1,0:T(2,128)(2,1)S(1)} %reshape.28), channel_id=1, replica_groups=mesh['pr'=8,'pc'=4] {'pr'}, dimensions={0} | all-to-all | bytes 1048576 | tf_op jit(solution)/shard_map/all_to_all | solution.py:45
  26.8 0.7 reshape.29
  27.5 0.0 copy-start.1
  27.5 0.4 copy.27
  27.9 0.0 copy-start.4
  28.0 1.6 %copy.28 = bf16[256,64,16]{0,1,2:T(8,128)(2,1)} copy(bf16[256,64,16]{1,2,0:T(8,128)(2,1)S(1)} %bitcast.66) | data formatting | bytes 1048576 | tf_op jit(solution)/shard_map/all_to_all | solution.py:45
  29.6 0.0 all-gather.2.cloned.1.call-update
  29.6 0.0 copy-done.1
  29.6 0.3 fusion.27
  29.9 0.0 copy-done.4
  29.9 0.4 fusion.15
  30.4 1.6 %copy.22 = bf16[32,64,128]{1,0,2:T(8,128)(2,1)S(1)} copy(bf16[32,64,128]{2,1,0:T(8,128)(2,1)S(1)} %fusion.15) | data formatting | bytes 1048576 | tf_op jit(solution)/shard_map/convert_element_type | solution.py:25
  32.0 0.7 reshape.30
  32.7 12.1 %all_to_all.46 = bf16[8,2,16384]{2,1,0:T(2,128)(2,1)S(1)} all-to-all(bf16[8,2,16384]{2,1,0:T(2,128)(2,1)S(1)} %reshape.30), channel_id=1, replica_groups=mesh['pr'=8,'pc'=4] {'pr'}, dimensions={0} | all-to-all | bytes 1048576 | tf_op jit(solution)/shard_map/all_to_all | solution.py:46
  44.8 0.7 reshape.31
  45.5 0.4 copy.24
  45.9 28.9 %all-gather.2.cloned.1.call-done = bf16[256,256,16]{0,1,2:T(8,128)(2,1)} async-done(((bf16[256,64,16]{0,1,2:T(8,128)(2,1)}), bf16[256,256,16]{0,1,2:T(8,128)(2,1)}) %all-gather.2.cloned.1.call-update) | async-done | bytes 2097168 | tf_op jit(solution)/shard_map/all_gather | solution.py:50
  74.8 2.4 %fusion.18 = bf16[256,64,16]{0,1,2:T(8,128)(2,1)S(1)} fusion(bf16[256,256,16]{0,1,2:T(8,128)(2,1)} %all-gather.2.cloned.1.call-done, bf16[256,64,16]{1,2,0:T(8,128)(2,1)S(1)} %bitcast.61), kind=kOutput, calls=%fused_computation.26 | convolution fusion | flops 134742016 | bytes 3145728 | tf_op jit(solution)/shard_map/kid,kjd->ijd/dot_general | solution.py:48
  77.2 0.0 copy-start.5
  77.2 1.0 copy.30
  78.1 1.5 %reshape.32 = bf16[8,2,16384]{2,1,0:T(2,128)(2,1)} reshape(bf16[256,16,64]{2,1,0:T(8,128)(2,1)S(1)} %bitcast.64) | data formatting | bytes 1048576
  79.6 3.7 %all-to-all-start.2 = ((bf16[8,2,16384]{2,1,0:T(2,128)(2,1)}), bf16[8,2,16384]{2,1,0:T(2,128)(2,1)S(1)}, u32[]{:S(2)}, u32[]{:S(2)}) async-start(bf16[8,2,16384]{2,1,0:T(2,128)(2,1)} %reshape.32), calls=%async_computation.2 | async-start | bytes 1048576 | tf_op jit(solution)/shard_map/all_to_all | solution.py:55
  83.3 0.0 copy-done.5
  83.3 0.4 fusion.13
  83.8 9.3 %all-to-all-done.2 = bf16[8,2,16384]{2,1,0:T(2,128)(2,1)S(1)} async-done(((bf16[8,2,16384]{2,1,0:T(2,128)(2,1)}), bf16[8,2,16384]{2,1,0:T(2,128)(2,1)S(1)}, u32[]{:S(2)}, u32[]{:S(2)}) %all-to-all-start.2) | async-done | bytes 524320 | tf_op jit(solution)/shard_map/all_to_all | solution.py:55
  93.0 0.7 reshape.33
  93.7 0.2 convert_bitcast_fusion
  93.9 0.2 fusion.19
  94.1 0.4 multiply_reduce_fusion
  94.5 0.0 copy-start.3
  94.5 0.3 copy.31
  94.8 0.4 copy-done.3
  95.2 0.0 copy-start.2
  95.2 0.5 fusion.2
  95.6 0.3 copy-done.2
  95.9 1.3 %fusion.17 = bf16[32,64,128]{2,1,0:T(8,128)(2,1)} fusion(f32[32,64,128]{2,1,0:T(8,128)S(1)} %fusion.13, bf16[32,64,128]{1,2,0:T(8,128)(2,1)S(1)} %fusion.2, bf16[128,128]{1,0:T(8,128)(2,1)S(1)} %copy-done.2), kind=kOutput, calls=%fused_computation.25 | convolution fusion | flops 67633152 | bytes 2129920 | tf_op jit(solution)/shard_map/ijd,dc->ijc/dot_general | solution.py:35
  (2 shorter events, 0.0 us)
Async XLA Ops:
  6.5 1.0 %copy-start = (bf16[32,64,128]{2,1,0:T(8,128)(2,1)S(1)}, bf16[32,64,128]{2,1,0:T(8,128)(2,1)}, u32[]{:S(2)}) copy-start(bf16[32,64,128]{2,1,0:T(8,128)(2,1)} %param.8) | copy-start | bytes 1572868
  6.5 68.3 %all-gather.2.cloned.1.call-start = ((), (), s32[]{:S(2)}) async-start(), calls=%async_computation.3 | async-start | bytes 2621440 | tf_op jit(solution)/shard_map/all_gather | solution.py:50
  27.5 2.1 %copy-start.1 = (bf16[128,128]{1,0:T(8,128)(2,1)S(1)}, bf16[128,128]{1,0:T(8,128)(2,1)}, u32[]{:S(2)}) copy-start(bf16[128,128]{1,0:T(8,128)(2,1)} %param.10) | copy-start | bytes 98308
  27.9 2.0 %copy-start.4 = (bf16[128,128]{1,0:T(8,128)(2,1)S(1)}, bf16[128,128]{1,0:T(8,128)(2,1)}, u32[]{:S(2)}) copy-start(bf16[128,128]{1,0:T(8,128)(2,1)} %param.12) | copy-start | bytes 98308
  77.2 6.2 %copy-start.5 = (bf16[128,128]{1,0:T(8,128)(2,1)S(1)}, bf16[128,128]{1,0:T(8,128)(2,1)}, u32[]{:S(2)}) copy-start(bf16[128,128]{1,0:T(8,128)(2,1)} %param.15) | copy-start | bytes 98308
  79.6 13.4 %all-to-all-start.2 = ((bf16[8,2,16384]{2,1,0:T(2,128)(2,1)}), bf16[8,2,16384]{2,1,0:T(2,128)(2,1)S(1)}, u32[]{:S(2)}, u32[]{:S(2)}) async-start(bf16[8,2,16384]{2,1,0:T(2,128)(2,1)} %reshape.32), calls=%async_computation.2 | async-start | bytes 1048576 | tf_op jit(solution)/shard_map/all_to_all | solution.py:55
  94.5 0.7 copy-start.3
  95.2 0.8 copy-start.2
Sparse Core Ops, SparseCore 0:
  29.7 45.0 all-gather.1
where the time goes:
time: 105 us; the launch traced here: 104 us
  waiting for transfers between devices  38.2 us (36%)
  blocking collectives  26.8 us (26%)
  between operations  13.6 us (13%)
  local copies, waits for them, and re-layouts  13.5 us (13%)
  matrix products  6.96 us (7%)
  starting transfers between devices  3.68 us (4%)
  other arithmetic  1.27 us (1%)
    all_gather x1, waiting for transfers between devices, on_device(): lax.all_gather(left_lines, 'pc', axis=1, tiled=True)  28.9 us
    all_to_all x1, blocking collectives, on_device(): lax.all_to_all(left, 'pr', split_axis=2, concat_axis=0, tiled=True)  14.7 us
    all_to_all x1, blocking collectives, on_device(): lax.all_to_all(right, 'pr', split_axis=2, concat_axis=0, tiled=True)  12.1 us
    all_to_all x1, waiting for transfers between devices, on_device(): mixed = lax.all_to_all(strip, 'pr', split_axis=0, concat_axis=2, tiled=True)  9.25 us
    unnamed x18, local copies, waits for them, and re-layouts  6.59 us
    all_to_all x1, starting transfers between devices, on_device(): mixed = lax.all_to_all(strip, 'pr', split_axis=0, concat_axis=2, tiled=True)  3.67 us
    convert_element_type x2, local copies, waits for them, and re-layouts, make_factors(): return (pair_in, left.astype(jnp.bfloat16), right.astype(jnp.bfloat16))  3.24 us
    dot_general x1, matrix products, on_device(): jnp.einsum('kid,kjd->ijd', lax.all_gather(left_lines, 'pc', axis=1, tiled...  2.35 us
  transfers between devices with their start and end apart: 2, of which 2 were waited for; matrix products, arithmetic and copies ran while one was open for 4% of the time, Pallas kernels for 0%

commit v1 on v0

--- a/solution.py
+++ b/solution.py
@@ -2,6 +2,13 @@
 import jax.numpy as jnp
 from jax import lax
 from jax.sharding import PartitionSpec as P
+
+
+def note_group(row_data, dim_at):
+    small = jnp.stack([row_data for _ in range(lax.axis_size("pc"))], 0)
+    work_now = lax.all_to_all(small, axis_name="pc", split_axis=0, concat_axis=0)
+    m_next = jnp.concatenate(work_now, dim_at)
+    return m_next
 
 
 def unit_channels(values, channel_gain):
@@ -46,10 +53,7 @@
         lax.all_to_all(right, "pr", split_axis=2, concat_axis=0, tiled=True),
     )
     strip = jnp.einsum(
-        "kid,kjd->ijd",
-        lax.all_gather(left_lines, "pc", axis=1, tiled=True),
-        right_lines,
-        preferred_element_type=jnp.float32,
+        "kid,kjd->ijd", note_group(left_lines, 1), right_lines, preferred_element_type=jnp.float32
     )
     strip = (strip * count ** (-0.5)).astype(jnp.bfloat16)
     mixed = lax.all_to_all(strip, "pr", split_axis=0, concat_axis=2, tiled=True)

time: 105 us -> 111 us (1.057)
  waiting for transfers between devices: 38.2 us -> 67.3 us
  blocking collectives: 26.8 us -> 0 us
  starting transfers between devices: 3.68 us -> 17.9 us
  between operations: 13.6 us -> 0.21 us
  local copies, waits for them, and re-layouts: 13.5 us -> 16.3 us
    all_to_all x0 -> x3, waiting for transfers between devices: none -> 58 us  [the longest x1 45 us: note_group(): lax.all_to_all(small, axis_name='pc', split_axis=0, concat_axis=0)]
    all_gather x1 -> x0, waiting for transfers between devices: 28.9 us -> none  [on_device(): lax.all_gather(left_lines, 'pc', axis=1, tiled=True)]
    all_to_all x2 -> x0, blocking collectives: 26.8 us -> none  [the longest x1 14.7 us: on_device(): lax.all_to_all(left, 'pr', split_axis=2, concat_axis=0, tiled=True)]
    all_to_all x0 -> x3, starting transfers between devices: none -> 13.6 us  [the longest x1 5.18 us: on_device(): lax.all_to_all(left, 'pr', split_axis=2, concat_axis=0, tiled=True)]
    another operation x0 -> x2, local copies, waits for them, and re-layouts: none -> 2.81 us  [note_group(): small = jnp.stack([row_data for _ in range(lax.axis_size('pc'))], 0)]
    all_to_all x2 -> x1, local copies, waits for them, and re-layouts: 2.06 us -> 0.41 us  [on_device(): lax.all_to_all(left, 'pr', split_axis=2, concat_axis=0, tiled=True)]
    unnamed x18, local copies, waits for them, and re-layouts: 6.59 us -> 8.2 us
  transfers between devices with their start and end apart: 2 -> 4, of which waited for: 2 -> 4; matrix products, arithmetic and copies ran while one was open for 4% -> 7% of each run, Pallas kernels for 0% -> 0%
where the time goes in v1:
time: 111 us; the launch traced here: 110 us
  waiting for transfers between devices  67.3 us (61%)
  starting transfers between devices  17.9 us (16%)
  local copies, waits for them, and re-layouts  16.3 us (15%)
  matrix products  7.16 us (6%)
  other arithmetic  1.27 us (1%)
    all_to_all x1, waiting for transfers between devices, note_group(): lax.all_to_all(small, axis_name='pc', split_axis=0, concat_axis=0)  45 us
    all_to_all x1, waiting for transfers between devices, on_device(): mixed = lax.all_to_all(strip, 'pr', split_axis=0, concat_axis=2, tiled=True)  9.28 us
    unnamed x18, local copies, waits for them, and re-layouts  8.2 us
    all_to_all x1, waiting for transfers between devices, on_device(): lax.all_to_all(right, 'pr', split_axis=2, concat_axis=0, tiled=True)  7.22 us
    all_to_all x1, waiting for transfers between devices, on_device(): lax.all_to_all(left, 'pr', split_axis=2, concat_axis=0, tiled=True)  5.83 us
    all_to_all x1, starting transfers between devices, on_device(): lax.all_to_all(left, 'pr', split_axis=2, concat_axis=0, tiled=True)  5.18 us
    all_to_all x1, starting transfers between devices, note_group(): lax.all_to_all(small, axis_name='pc', split_axis=0, concat_axis=0)  4.87 us
    all_to_all x1, starting transfers between devices, on_device(): mixed = lax.all_to_all(strip, 'pr', split_axis=0, concat_axis=2, tiled=True)  4.31 us
  transfers between devices with their start and end apart: 4, of which 4 were waited for; matrix products, arithmetic and copies ran while one was open for 7% of the time, Pallas kernels for 0%

profile of v1, /device:TPU:0, one launch (start us, length us, event | category | flops | bytes accessed | tf_op | source)
XLA Modules:
  0.0 110.1 jit_solution(14420731460168739265)
XLA Ops:
  0.0 0.0 copy-start
  0.0 1.0 copy-done
  1.0 1.0 fusion.33
  2.1 1.2 %fusion.19 = bf16[32,64,128]{2,1,0:T(8,128)(2,1)S(1)} fusion(f32[32,64,128]{2,1,0:T(8,128)S(1)} %fusion.33, bf16[32,64,128]{2,1,0:T(8,128)(2,1)S(1)} %copy-done, bf16[128,128]{1,0:T(8,128)(2,1)} %param.11), kind=kOutput, calls=%fused_computation.24 | convolution fusion | flops 68419584 | bytes 2129920 | tf_op jit(solution)/shard_map/ijc,cd->ijd/dot_general | solution.py:26
  3.3 0.0 copy-start.1
  3.3 1.6 %copy.25 = bf16[32,64,128]{1,0,2:T(8,128)(2,1)S(1)} copy(bf16[32,64,128]{2,1,0:T(8,128)(2,1)S(1)} %fusion.19) | data formatting | bytes 1048576 | tf_op jit(solution)/shard_map/convert_element_type | solution.py:32
  4.9 0.0 copy-start.4
  4.9 1.5 %reshape.39 = bf16[8,2,16384]{2,1,0:T(2,128)(2,1)} reshape(bf16[128,32,64]{2,1,0:T(8,128)(2,1)S(1)} %bitcast.63) | data formatting | bytes 1048576
  6.4 5.2 %all-to-all-start.1 = ((bf16[8,2,16384]{2,1,0:T(2,128)(2,1)}), bf16[8,2,16384]{2,1,0:T(2,128)(2,1)S(1)}, u32[]{:S(2)}, u32[]{:S(2)}) async-start(bf16[8,2,16384]{2,1,0:T(2,128)(2,1)} %reshape.39), calls=%async_computation.1 | async-start | bytes 1048576 | tf_op jit(solution)/shard_map/all_to_all | solution.py:52
  11.6 0.0 copy-done.1
  11.6 0.3 fusion.36
  11.9 0.0 copy-done.4
  11.9 0.4 fusion.20
  12.4 1.6 %copy.22 = bf16[32,64,128]{1,0,2:T(8,128)(2,1)S(1)} copy(bf16[32,64,128]{2,1,0:T(8,128)(2,1)S(1)} %fusion.20) | data formatting | bytes 1048576 | tf_op jit(solution)/shard_map/convert_element_type | solution.py:32
  14.0 1.5 %reshape.41 = bf16[8,2,16384]{2,1,0:T(2,128)(2,1)} reshape(bf16[128,32,64]{2,1,0:T(8,128)(2,1)S(1)} %bitcast.64) | data formatting | bytes 1048576
  15.5 5.8 %all-to-all-done.1 = bf16[8,2,16384]{2,1,0:T(2,128)(2,1)S(1)} async-done(((bf16[8,2,16384]{2,1,0:T(2,128)(2,1)}), bf16[8,2,16384]{2,1,0:T(2,128)(2,1)S(1)}, u32[]{:S(2)}, u32[]{:S(2)}) %all-to-all-start.1) | async-done | bytes 524320 | tf_op jit(solution)/shard_map/all_to_all | solution.py:52
  21.3 3.5 %all-to-all-start = ((bf16[8,2,16384]{2,1,0:T(2,128)(2,1)}), bf16[8,2,16384]{2,1,0:T(2,128)(2,1)S(1)}, u32[]{:S(2)}, u32[]{:S(2)}) async-start(bf16[8,2,16384]{2,1,0:T(2,128)(2,1)} %reshape.41), calls=%async_computation | async-start | bytes 1048576 | tf_op jit(solution)/shard_map/all_to_all | solution.py:53
  24.8 0.7 reshape.40
  25.5 0.4 copy.27
  25.9 1.3 %copy.28 = bf16[256,64,16]{0,2,1:T(8,128)(2,1)S(1)} copy(bf16[256,64,16]{1,2,0:T(8,128)(2,1)S(1)} %bitcast.67) | data formatting | bytes 1048576 | tf_op jit(solution)/shard_map/stack | solution.py:8
  27.3 7.2 %all-to-all-done = bf16[8,2,16384]{2,1,0:T(2,128)(2,1)S(1)} async-done(((bf16[8,2,16384]{2,1,0:T(2,128)(2,1)}), bf16[8,2,16384]{2,1,0:T(2,128)(2,1)S(1)}, u32[]{:S(2)}, u32[]{:S(2)}) %all-to-all-start) | async-done | bytes 524320 | tf_op jit(solution)/shard_map/all_to_all | solution.py:53
  34.5 1.5 %stack.10 = bf16[4,256,64,16]{1,3,2,0:T(8,128)(2,1)} broadcast(bf16[256,64,16]{0,2,1:T(8,128)(2,1)S(1)} %copy.28), dimensions={1,2,3} | broadcast | bytes 2621440 | tf_op jit(solution)/shard_map/stack | solution.py:8
  36.0 4.9 %all-to-all-start.2 = ((bf16[4,256,64,16]{1,3,2,0:T(8,128)(2,1)}), bf16[4,256,64,16]{1,3,2,0:T(8,128)(2,1)}, u32[]{:S(2)}, u32[]{:S(2)}) async-start(bf16[4,256,64,16]{1,3,2,0:T(8,128)(2,1)} %stack.10), calls=%async_computation.2 | async-start | bytes 4194304 | tf_op jit(solution)/shard_map/all_to_all | solution.py:9
  40.8 0.7 reshape.42
  41.5 0.4 copy.24
  41.9 45.0 %all-to-all-done.2 = bf16[4,256,64,16]{1,3,2,0:T(8,128)(2,1)} async-done(((bf16[4,256,64,16]{1,3,2,0:T(8,128)(2,1)}), bf16[4,256,64,16]{1,3,2,0:T(8,128)(2,1)}, u32[]{:S(2)}, u32[]{:S(2)}) %all-to-all-start.2) | async-done | bytes 2097184 | tf_op jit(solution)/shard_map/all_to_all | solution.py:9
  86.9 2.5 %fusion.25 = bf16[256,64,16]{0,1,2:T(8,128)(2,1)S(1)} fusion(bf16[256,256,16]{0,2,1:T(8,128)(2,1)} %bitcast.13, bf16[256,64,16]{1,2,0:T(8,128)(2,1)S(1)} %bitcast.69), kind=kOutput, calls=%fused_computation.28 | convolution fusion | flops 134742016 | bytes 3145728 | tf_op jit(solution)/shard_map/kid,kjd->ijd/dot_general | solution.py:55
  89.4 0.0 copy-start.5
  89.4 1.0 copy.31
  90.4 1.5 %reshape.43 = bf16[8,2,16384]{2,1,0:T(2,128)(2,1)} reshape(bf16[256,16,64]{2,1,0:T(8,128)(2,1)S(1)} %bitcast.65) | data formatting | bytes 1048576
  91.9 4.3 %all-to-all-start.3 = ((bf16[8,2,16384]{2,1,0:T(2,128)(2,1)}), bf16[8,2,16384]{2,1,0:T(2,128)(2,1)S(1)}, u32[]{:S(2)}, u32[]{:S(2)}) async-start(bf16[8,2,16384]{2,1,0:T(2,128)(2,1)} %reshape.43), calls=%async_computation.3 | async-start | bytes 1048576 | tf_op jit(solution)/shard_map/all_to_all | solution.py:59
  96.2 0.0 copy-done.5
  96.2 0.4 fusion.18
  96.6 9.3 %all-to-all-done.3 = bf16[8,2,16384]{2,1,0:T(2,128)(2,1)S(1)} async-done(((bf16[8,2,16384]{2,1,0:T(2,128)(2,1)}), bf16[8,2,16384]{2,1,0:T(2,128)(2,1)S(1)}, u32[]{:S(2)}, u32[]{:S(2)}) %all-to-all-start.3) | async-done | bytes 524320 | tf_op jit(solution)/shard_map/all_to_all | solution.py:59
  105.9 0.7 reshape.44
  106.6 0.2 convert_bitcast_fusion
  106.8 0.2 fusion.28
  107.0 0.4 multiply_reduce_fusion
  107.4 0.0 copy-start.3
  107.4 0.3 copy.32
  107.7 0.4 copy-done.3
  108.1 0.0 copy-start.2
  108.1 0.5 fusion.2
  108.5 0.3 copy-done.2
  108.8 1.3 %fusion.21 = bf16[32,64,128]{2,1,0:T(8,128)(2,1)} fusion(f32[32,64,128]{2,1,0:T(8,128)S(1)} %fusion.18, bf16[32,64,128]{1,2,0:T(8,128)(2,1)S(1)} %fusion.2, bf16[128,128]{1,0:T(8,128)(2,1)S(1)} %copy-done.2), kind=kOutput, calls=%fused_computation.26 | convolution fusion | flops 67633152 | bytes 2129920 | tf_op jit(solution)/shard_map/ijd,dc->ijc/dot_general | solution.py:42
  (2 shorter events, 0.0 us)
Async XLA Ops:
  0.0 1.0 copy-start
  3.3 8.3 %copy-start.1 = (bf16[128,128]{1,0:T(8,128)(2,1)S(1)}, bf16[128,128]{1,0:T(8,128)(2,1)}, u32[]{:S(2)}) copy-start(bf16[128,128]{1,0:T(8,128)(2,1)} %param.10) | copy-start | bytes 98308
  4.9 7.0 %copy-start.4 = (bf16[128,128]{1,0:T(8,128)(2,1)S(1)}, bf16[128,128]{1,0:T(8,128)(2,1)}, u32[]{:S(2)}) copy-start(bf16[128,128]{1,0:T(8,128)(2,1)} %param.12) | copy-start | bytes 98308
  6.4 14.9 %all-to-all-start.1 = ((bf16[8,2,16384]{2,1,0:T(2,128)(2,1)}), bf16[8,2,16384]{2,1,0:T(2,128)(2,1)S(1)}, u32[]{:S(2)}, u32[]{:S(2)}) async-start(bf16[8,2,16384]{2,1,0:T(2,128)(2,1)} %reshape.39), calls=%async_computation.1 | async-start | bytes 1048576 | tf_op jit(solution)/shard_map/all_to_all | solution.py:52
  21.3 13.1 %all-to-all-start = ((bf16[8,2,16384]{2,1,0:T(2,128)(2,1)}), bf16[8,2,16384]{2,1,0:T(2,128)(2,1)S(1)}, u32[]{:S(2)}, u32[]{:S(2)}) async-start(bf16[8,2,16384]{2,1,0:T(2,128)(2,1)} %reshape.41), calls=%async_computation | async-start | bytes 1048576 | tf_op jit(solution)/shard_map/all_to_all | solution.py:53
  36.0 50.9 %all-to-all-start.2 = ((bf16[4,256,64,16]{1,3,2,0:T(8,128)(2,1)}), bf16[4,256,64,16]{1,3,2,0:T(8,128)(2,1)}, u32[]{:S(2)}, u32[]{:S(2)}) async-start(bf16[4,256,64,16]{1,3,2,0:T(8,128)(2,1)} %stack.10), calls=%async_computation.2 | async-start | bytes 4194304 | tf_op jit(solution)/shard_map/all_to_all | solution.py:9
  89.4 6.8 %copy-start.5 = (bf16[128,128]{1,0:T(8,128)(2,1)S(1)}, bf16[128,128]{1,0:T(8,128)(2,1)}, u32[]{:S(2)}) copy-start(bf16[128,128]{1,0:T(8,128)(2,1)} %param.15) | copy-start | bytes 98308
  91.9 14.0 %all-to-all-start.3 = ((bf16[8,2,16384]{2,1,0:T(2,128)(2,1)}), bf16[8,2,16384]{2,1,0:T(2,128)(2,1)S(1)}, u32[]{:S(2)}, u32[]{:S(2)}) async-start(bf16[8,2,16384]{2,1,0:T(2,128)(2,1)} %reshape.43), calls=%async_computation.3 | async-start | bytes 1048576 | tf_op jit(solution)/shard_map/all_to_all | solution.py:59
  107.4 0.7 copy-start.3
  108.1 0.8 copy-start.2
